TPU v7x, 32 devices: a whole 2x2x4 slice. The times are simulated.
32 devices in a mesh: silo: 4 (over z), row: 8 (over y, x, core).
Axes of the slice: x: 2, y: 2, z: 4, core: 2. Of those that a mesh axis runs over, the one named last changes fastest.
Arguments:
- silo_grams: float32 [8, 4096, 4096], P('silo', 'row'), may hold values from -9 to 81, as said below
- silo_weights: bfloat16 [8, 4096, 640], P('silo', 'row'), may hold values from -6 to 6
Outputs:
- merged_rows: float32 [640, 4096], P(('silo', 'row'))
Inputs may be any that keep to these rules, and one draw needn't show every extreme that they name: `silo_grams`: each silo's Gram is symmetric up to float32 rounding and positive definite.
All inputs are finite; a program needn't handle non-finite values.
Results may differ from a plain program's by a relative error of at most 0.0003.
Values may be sent and summed in bfloat16 or wider, within the bound.
No kernel may reach another device: no remote copies, remote signals or barrier semaphores. Data moves between devices by JAX's collectives and lax.ppermute only.
A program may use at most 128 MiB of HBM per device.

v0:
```python
import jax
import jax.numpy as jnp
from jax import lax
from jax.sharding import PartitionSpec as P

ITERS = 2
full_precision = lax.Precision.HIGHEST


def conj_grad(right_side, apply_op, sum_squares, sum_curv):
    solution = jnp.zeros_like(right_side)
    residual = right_side
    direction = right_side
    res_norm = sum_squares(jnp.sum(residual * residual, axis=0))
    for iteration in range(ITERS):
        mapped = apply_op(direction)
        step_size = res_norm / sum_curv(jnp.sum(direction * mapped, axis=0))
        solution = solution + step_size * direction
        residual = residual - step_size * mapped
        if iteration + 1 < ITERS:
            next_norm = sum_squares(jnp.sum(residual * residual, axis=0))
            direction = residual + next_norm / res_norm * direction
            res_norm = next_norm
    return solution


def local(silo_grams, silo_weights):
    partial_op = jnp.sum(silo_grams, axis=0)
    partial_rhs = jnp.einsum(
        "srk,skc->rc",
        silo_grams,
        lax.all_gather(silo_weights, "row", axis=1, tiled=True).astype(jnp.float32),
        precision=full_precision,
    )
    operator = lax.psum(partial_op, "silo")
    right_side = lax.psum_scatter(partial_rhs, "silo", scatter_dimension=1, tiled=True)

    def apply_cols(direction):
        return jnp.dot(
            operator, lax.all_gather(direction, "row", axis=0, tiled=True), precision=full_precision
        )

    def squares_cols(values):
        return lax.psum(values, "row")

    def curv_values(values):
        return lax.psum(values, "row")

    solution = conj_grad(right_side, apply_cols, squares_cols, curv_values)
    transposed = solution.T
    return lax.all_to_all(transposed, "row", split_axis=0, concat_axis=1, tiled=True)


def solution(mesh):
    placed = (P("silo", "row", None), P("silo", "row", None))
    return jax.shard_map(
        local, mesh=mesh, in_specs=placed, out_specs=P(("silo", "row"), None), check_vma=False
    )
```

profile of v0, /device:TPU:0, one launch (start us, length us, event | category | flops | bytes accessed | tf_op | source)
XLA Modules:
  0.0 567.5 jit_solution(10931932025676428913)
XLA Ops:
  6.5 0.0 all-gather.4.cloned.1.call-start
  6.5 2.4 copy.6
  9.0 0.0 all-gather.4.cloned.1.call-update
  9.0 0.0 reduce-scatter.2.cloned.1.call-start
  9.0 68.1 %all-gather.4.cloned.1.call-done = bf16[2,4096,640]{1,2,0:T(8,128)(2,1)} async-done(((bf16[2,512,640]{1,2,0:T(8,128)(2,1)}), bf16[2,4096,640]{1,2,0:T(8,128)(2,1)}) %all-gather.4.cloned.1.call-update) | async-done | bytes 10485776 | tf_op jit(solution)/shard_map/all_gather | solution.py:32
  77.1 21.3 %convolution_bitcast_fusion = f32[512,640]{0,1:T(8,128)} fusion(f32[2,512,4096]{2,1,0:T(8,128)} %param.2, bf16[2,4096,640]{1,2,0:T(8,128)(2,1)} %all-gather.4.cloned.1.call-done), kind=kOutput, calls=%fused_computation | convolution fusion | flops 32212254720 | bytes 28573696 | tf_op jit(solution)/shard_map/srk,skc->rc/dot_general | solution.py:29
  98.4 0.0 reduce-scatter.2.cloned.1.call-update
  98.5 0.0 all-reduce.3.cloned.1.call-start
  98.5 11.6 %reduce_sum.46 = f32[512,4096]{1,0:T(8,128)} reduce(f32[2,512,4096]{2,1,0:T(8,128)} %param.2, f32[]{:T(128)} %constant.0.clone.1), dimensions={0}, to_apply=%region_3.0 | reduce | flops 2097152 | bytes 25165828 | tf_op jit(solution)/shard_map/reduce_sum | solution.py:28
  110.1 0.0 all-reduce.3.cloned.1.call-update
  110.1 0.0 all-gather.6.cloned.1.call-start
  110.2 19.8 %reduce-scatter.2.cloned.1.call-done = f32[512,160]{0,1:T(8,128)} async-done(((f32[512,640]{0,1:T(8,128)}), f32[512,160]{0,1:T(8,128)}) %reduce-scatter.2.cloned.1.call-update) | async-done | bytes 327696 | tf_op jit(solution)/shard_map/reduce_scatter | solution.py:36
  130.0 0.0 copy-start
  130.0 0.0 all-gather.6.cloned.1.call-update
  130.0 0.2 all-gather.8.cloned.1.call-start
  130.2 291.8 %all-reduce.3.cloned.1.call-done = f32[512,4096]{1,0:T(8,128)} async-done(((f32[512,4096]{1,0:T(8,128)}), f32[512,4096]{1,0:T(8,128)}) %all-reduce.3.cloned.1.call-update) | async-done | bytes 8388624 | tf_op jit(solution)/shard_map/psum | solution.py:35
  422.0 30.8 %all-gather.6.cloned.1.call-done = f32[4096,160]{0,1:T(8,128)} async-done(((f32[512,160]{0,1:T(8,128)}), f32[4096,160]{0,1:T(8,128)}) %all-gather.6.cloned.1.call-update) | async-done | bytes 2621456 | tf_op jit(solution)/shard_map/all_gather | solution.py:40
  452.8 13.3 %multiply_reduce_fusion.1 = (f32[160]{0:T(256)S(1)}, f32[160]{0:T(256)S(1)}, f32[512,160]{0,1:T(8,128)S(1)}) fusion(f32[512,160]{0,1:T(8,128)} %reduce-scatter.2.cloned.1.call-done, f32[512,4096]{1,0:T(8,128)} %all-reduce.3.cloned.1.call-done, f32[4096,160]{0,1:T(8,128)} %all-gather.6.cloned.1.call-done), kind=kOutput, calls=%fused_computation.7 | convolution fusion | flops 4026859264 | bytes 11666688 | tf_op jit(solution)/shard_map/dot_general | solution.py:39
  466.0 13.1 %all-reduce = (f32[160]{0:T(256)S(1)}, f32[160]{0:T(256)S(1)}) all-reduce(f32[160]{0:T(256)S(1)} %get-tuple-element.6, f32[160]{0:T(256)S(1)} %get-tuple-element.5), channel_id=1, replica_groups=mesh['silo'=4,'row'=8] {'row'}, use_global_device_ids=true, to_apply=%region_2.0 | all-reduce | flops 320 | bytes 2560 | tf_op jit(solution)/shard_map/psum | solution.py:44
  479.1 0.0 copy-done
  479.1 0.2 multiply_reduce_fusion
  479.3 12.0 %psum.38 = f32[160]{0:T(256)S(1)} all-reduce(f32[160]{0:T(256)S(1)} %multiply_reduce_fusion), channel_id=1, replica_groups=mesh['silo'=4,'row'=8] {'row'}, use_global_device_ids=true, to_apply=%region_8.0 | all-reduce | flops 160 | bytes 1280 | tf_op jit(solution)/shard_map/psum | solution.py:44
  491.4 0.9 multiply_add_fusion
  492.2 0.0 copy-start.1
  492.2 0.0 all-gather.8.cloned.1.call-update
  492.3 30.1 %all-gather.8.cloned.1.call-done = f32[4096,160]{0,1:T(8,128)} async-done(((f32[512,160]{0,1:T(8,128)}), f32[4096,160]{0,1:T(8,128)}) %all-gather.8.cloned.1.call-update) | async-done | bytes 2621456 | tf_op jit(solution)/shard_map/all_gather | solution.py:40
  522.4 13.2 %fusion = f32[160]{0:T(256)S(1)} fusion(f32[512,160]{0,1:T(8,128)} %multiply_add_fusion, f32[512,4096]{1,0:T(8,128)} %all-reduce.3.cloned.1.call-done, f32[4096,160]{0,1:T(8,128)} %all-gather.8.cloned.1.call-done), kind=kOutput, calls=%fused_computation.2 | convolution fusion | flops 4026695680 | bytes 11338368 | tf_op jit(solution)/shard_map/dot_general | solution.py:39
  535.7 13.1 %psum.39 = f32[160]{0:T(256)S(1)} all-reduce(f32[160]{0:T(256)S(1)} %fusion), channel_id=1, replica_groups=mesh['silo'=4,'row'=8] {'row'}, use_global_device_ids=true, to_apply=%region_10.0 | all-reduce | flops 160 | bytes 1280 | tf_op jit(solution)/shard_map/psum | solution.py:47
  548.7 0.0 copy-done.1
  548.8 0.1 add_bitcast_fusion
  548.9 10.9 %all_to_all.19 = f32[8,20,512]{2,1,0:T(8,128)S(1)} all-to-all(f32[8,20,512]{2,1,0:T(8,128)S(1)} %all_to_all.14), channel_id=1, replica_groups=mesh['silo'=4,'row'=8] {'row'}, dimensions={0} | all-to-all | bytes 655360 | tf_op jit(solution)/shard_map/all_to_all | solution.py:51
  559.8 0.2 copy.7
  560.0 1.0 copy.8
  (5 shorter events, 0.1 us)
Async XLA Ops:
  6.5 70.6 %all-gather.4.cloned.1.call-start = ((), (), s32[]{:S(2)}) async-start(), calls=%async_computation.2 | async-start | bytes 11796480 | tf_op jit(solution)/shard_map/all_gather | solution.py:32
  9.0 121.0 %reduce-scatter.2.cloned.1.call-start = ((), (), s32[]{:S(2)}) async-start(), calls=%async_computation.3 | async-start | bytes 1638400 | tf_op jit(solution)/shard_map/reduce_scatter | solution.py:36
  98.5 323.5 %all-reduce.3.cloned.1.call-start = ((), (), s32[]{:S(2)}) async-start(), calls=%async_computation.4 | async-start | bytes 16777216 | tf_op jit(solution)/shard_map/psum | solution.py:35
  110.1 342.7 %all-gather.6.cloned.1.call-start = ((), (), s32[]{:S(2)}) async-start(), calls=%async_computation.5 | async-start | bytes 2949120 | tf_op jit(solution)/shard_map/all_gather | solution.py:40
  130.0 349.2 %copy-start = (f32[512,160]{0,1:T(8,128)S(1)}, f32[512,160]{0,1:T(8,128)}, u32[]{:S(2)}) copy-start(f32[512,160]{0,1:T(8,128)} %reduce-scatter.2.cloned.1.call-done) | copy-start | bytes 983044
  130.0 392.4 %all-gather.8.cloned.1.call-start = ((), (), s32[]{:S(2)}) async-start(), calls=%async_computation.6 | async-start | bytes 2949120 | tf_op jit(solution)/shard_map/all_gather | solution.py:40
  492.2 56.5 %copy-start.1 = (f32[512,160]{0,1:T(8,128)S(1)}, f32[512,160]{0,1:T(8,128)}, u32[]{:S(2)}) copy-start(f32[512,160]{0,1:T(8,128)} %multiply_add_fusion) | copy-start | bytes 983044
Sparse Core Ops, SparseCore 0:
  9.2 67.8 all-gather.3
  98.6 31.3 reduce-scatter.1
  132.5 289.4 all-reduce.2
  423.8 28.9 all-gather.5
  492.4 29.9 all-gather.7
where the time goes:
time: 568 us
  waiting for transfers between devices  441 us (78%)
  blocking collectives  49 us (9%)
  matrix products  47.8 us (8%)
  between operations  13.2 us (2%)
  other arithmetic  12.8 us (2%)
    psum x1, waiting for transfers between devices, local(): operator = lax.psum(partial_op, 'silo')  292 us
    all_gather x1, waiting for transfers between devices, local(): lax.all_gather(silo_weights, 'row', axis=1, tiled=True).astype(jnp.float32)  68.1 us
    all_gather x2, waiting for transfers between devices, apply_cols(): lax.all_gather(direction, 'row', axis=0, tiled=True)  60.9 us
    dot_general x2, matrix products, apply_cols(): jnp.dot(operator, lax.all_gather(direction, 'row', axis=0, tiled=True), p...  26.5 us
    psum x2, blocking collectives, squares_cols(): return lax.psum(values, 'row')  25.1 us
    dot_general x1, matrix products, local(): jnp.einsum('srk,skc->rc', silo_grams, lax.all_gather(silo_weights, 'row',...  21.3 us
    reduce_scatter x1, waiting for transfers between devices, local(): lax.psum_scatter(partial_rhs, 'silo', scatter_dimension=1, tiled=True)  19.8 us
    psum x1, blocking collectives, curv_values(): return lax.psum(values, 'row')  13.1 us
  transfers between devices with their start and end apart: 5, of which 5 were waited for; matrix products, arithmetic and copies ran while one was open for 2% of the time, Pallas kernels for 0%

commit v1 on v0

--- a/solution.py
+++ b/solution.py
@@ -32,7 +32,7 @@
         lax.all_gather(silo_weights, "row", axis=1, tiled=True).astype(jnp.float32),
         precision=full_precision,
     )
-    operator = lax.psum(partial_op, "silo")
+    operator = jnp.sum(lax.all_gather(partial_op, "silo"), axis=0)
     right_side = lax.psum_scatter(partial_rhs, "silo", scatter_dimension=1, tiled=True)
 
     def apply_cols(direction):

time: 568 us -> 835 us (1.47)
  waiting for transfers between devices: 441 us -> 694 us
  other arithmetic: 12.8 us -> 28.6 us
    all_gather x0 -> x1, waiting for transfers between devices: none -> 562 us  [local(): operator = jnp.sum(lax.all_gather(partial_op, 'silo'), axis=0)]
    psum x1 -> x0, waiting for transfers between devices: 292 us -> none  [local(): operator = lax.psum(partial_op, 'silo')]
    all_gather x2, waiting for transfers between devices: 60.9 us -> 44.3 us  [apply_cols(): lax.all_gather(direction, 'row', axis=0, tiled=True)]
    reduce_sum x0 -> x1, other arithmetic: none -> 15.8 us  [local(): operator = jnp.sum(lax.all_gather(partial_op, 'silo'), axis=0)]
  transfers between devices with their start and end apart: 5 -> 5, of which waited for: 5 -> 5; matrix products, arithmetic and copies ran while one was open for 2% -> 3% of each run, Pallas kernels for 0% -> 0%
where the time goes in v1:
time: 835 us
  waiting for transfers between devices  694 us (83%)
  blocking collectives  49 us (6%)
  matrix products  46.7 us (6%)
  other arithmetic  28.6 us (3%)
  between operations  13.2 us (2%)
    all_gather x1, waiting for transfers between devices, local(): operator = jnp.sum(lax.all_gather(partial_op, 'silo'), axis=0)  562 us
    all_gather x1, waiting for transfers between devices, local(): lax.all_gather(silo_weights, 'row', axis=1, tiled=True).astype(jnp.float32)  68.1 us
    all_gather x2, waiting for transfers between devices, apply_cols(): lax.all_gather(direction, 'row', axis=0, tiled=True)  44.3 us
    dot_general x2, matrix products, apply_cols(): jnp.dot(operator, lax.all_gather(direction, 'row', axis=0, tiled=True), p...  25.4 us
    psum x2, blocking collectives, squares_cols(): return lax.psum(values, 'row')  25.1 us
    dot_general x1, matrix products, local(): jnp.einsum('srk,skc->rc', silo_grams, lax.all_gather(silo_weights, 'row',...  21.3 us
    reduce_scatter x1, waiting for transfers between devices, local(): lax.psum_scatter(partial_rhs, 'silo', scatter_dimension=1, tiled=True)  19.8 us
  transfers between devices with their start and end apart: 5, of which 5 were waited for; matrix products, arithmetic and copies ran while one was open for 3% of the time, Pallas kernels for 0%

profile of v1, /device:TPU:0, one launch (start us, length us, event | category | flops | bytes accessed | tf_op | source)
XLA Modules:
  0.0 835.2 jit_solution(229290111698581191)
XLA Ops:
  6.5 0.0 all-gather.6.cloned.1.call-start
  6.5 2.4 copy.8
  9.0 0.0 all-gather.6.cloned.1.call-update
  9.0 0.0 reduce-scatter.2.cloned.1.call-start
  9.0 68.1 %all-gather.6.cloned.1.call-done = bf16[2,4096,640]{1,2,0:T(8,128)(2,1)} async-done(((bf16[2,512,640]{1,2,0:T(8,128)(2,1)}), bf16[2,4096,640]{1,2,0:T(8,128)(2,1)}) %all-gather.6.cloned.1.call-update) | async-done | bytes 10485776 | tf_op jit(solution)/shard_map/all_gather | solution.py:32
  77.1 21.3 %convolution_bitcast_fusion = f32[512,640]{0,1:T(8,128)} fusion(f32[2,512,4096]{2,1,0:T(8,128)} %param.2, bf16[2,4096,640]{1,2,0:T(8,128)(2,1)} %all-gather.6.cloned.1.call-done), kind=kOutput, calls=%fused_computation | convolution fusion | flops 32212254720 | bytes 28573696 | tf_op jit(solution)/shard_map/srk,skc->rc/dot_general | solution.py:29
  98.5 0.0 reduce-scatter.2.cloned.1.call-update
  98.5 0.0 all-gather.12.cloned.1.call-start
  98.5 11.5 %reduce_sum.55 = f32[512,4096]{1,0:T(8,128)} reduce(f32[2,512,4096]{2,1,0:T(8,128)} %param.2, f32[]{:T(128)} %constant.0.clone.1), dimensions={0}, to_apply=%region_3.0 | reduce | flops 2097152 | bytes 25165828 | tf_op jit(solution)/shard_map/reduce_sum | solution.py:28
  110.1 0.0 all-gather.12.cloned.1.call-update
  110.1 0.0 all-gather.8.cloned.1.call-start
  110.1 19.8 %reduce-scatter.2.cloned.1.call-done = f32[512,160]{0,1:T(8,128)} async-done(((f32[512,640]{0,1:T(8,128)}), f32[512,160]{0,1:T(8,128)}) %reduce-scatter.2.cloned.1.call-update) | async-done | bytes 327696 | tf_op jit(solution)/shard_map/reduce_scatter | solution.py:36
  130.0 0.0 all-gather.8.cloned.1.call-update
  130.0 0.0 all-gather.10.cloned.1.call-start
  130.1 561.6 %all-gather.12.cloned.1.call-done = f32[2048,4096]{1,0:T(8,128)} async-done(((f32[512,4096]{1,0:T(8,128)}), f32[2048,4096]{1,0:T(8,128)}) %all-gather.12.cloned.1.call-update) | async-done | bytes 33554448 | tf_op jit(solution)/shard_map/all_gather | solution.py:35
  691.7 0.0 copy-start
  691.7 15.8 %reduce_sum.56 = f32[512,4096]{1,0:T(8,128)} reduce(f32[4,512,4096]{2,1,0:T(8,128)} %bitcast.15, f32[]{:T(128)} %constant.0.clone.1), dimensions={0}, to_apply=%region_4.0 | reduce | flops 6291456 | bytes 41943044 | tf_op jit(solution)/shard_map/reduce_sum | solution.py:35
  707.5 14.1 %all-gather.8.cloned.1.call-done = f32[4096,160]{0,1:T(8,128)} async-done(((f32[512,160]{0,1:T(8,128)}), f32[4096,160]{0,1:T(8,128)}) %all-gather.8.cloned.1.call-update) | async-done | bytes 2621456 | tf_op jit(solution)/shard_map/all_gather | solution.py:40
  721.6 0.0 copy-done
  721.6 12.1 %multiply_reduce_fusion.1 = (f32[160]{0:T(256)S(1)}, f32[160]{0:T(256)S(1)}, f32[512,160]{0,1:T(8,128)S(1)}) fusion(f32[512,160]{0,1:T(8,128)S(1)} %copy-done, f32[512,4096]{1,0:T(8,128)} %reduce_sum.56, f32[4096,160]{0,1:T(8,128)} %all-gather.8.cloned.1.call-done), kind=kOutput, calls=%fused_computation.7 | convolution fusion | flops 4026859264 | bytes 11666688 | tf_op jit(solution)/shard_map/dot_general | solution.py:39
  733.8 13.1 %all-reduce = (f32[160]{0:T(256)S(1)}, f32[160]{0:T(256)S(1)}) all-reduce(f32[160]{0:T(256)S(1)} %get-tuple-element.6, f32[160]{0:T(256)S(1)} %get-tuple-element.5), channel_id=1, replica_groups=mesh['silo'=4,'row'=8] {'row'}, use_global_device_ids=true, to_apply=%region_2.0 | all-reduce | flops 320 | bytes 2560 | tf_op jit(solution)/shard_map/psum | solution.py:44
  746.9 0.2 multiply_reduce_fusion
  747.1 12.0 %psum.30 = f32[160]{0:T(256)S(1)} all-reduce(f32[160]{0:T(256)S(1)} %multiply_reduce_fusion), channel_id=1, replica_groups=mesh['silo'=4,'row'=8] {'row'}, use_global_device_ids=true, to_apply=%region_8.0 | all-reduce | flops 160 | bytes 1280 | tf_op jit(solution)/shard_map/psum | solution.py:44
  759.0 0.9 multiply_add_fusion
  759.9 0.0 copy-start.1
  759.9 0.0 all-gather.10.cloned.1.call-update
  759.9 30.1 %all-gather.10.cloned.1.call-done = f32[4096,160]{0,1:T(8,128)} async-done(((f32[512,160]{0,1:T(8,128)}), f32[4096,160]{0,1:T(8,128)}) %all-gather.10.cloned.1.call-update) | async-done | bytes 2621456 | tf_op jit(solution)/shard_map/all_gather | solution.py:40
  790.1 13.2 %fusion = f32[160]{0:T(256)S(1)} fusion(f32[512,160]{0,1:T(8,128)} %multiply_add_fusion, f32[512,4096]{1,0:T(8,128)} %reduce_sum.56, f32[4096,160]{0,1:T(8,128)} %all-gather.10.cloned.1.call-done), kind=kOutput, calls=%fused_computation.2 | convolution fusion | flops 4026695680 | bytes 11338368 | tf_op jit(solution)/shard_map/dot_general | solution.py:39
  803.3 13.1 %psum.31 = f32[160]{0:T(256)S(1)} all-reduce(f32[160]{0:T(256)S(1)} %fusion), channel_id=1, replica_groups=mesh['silo'=4,'row'=8] {'row'}, use_global_device_ids=true, to_apply=%region_10.0 | all-reduce | flops 160 | bytes 1280 | tf_op jit(solution)/shard_map/psum | solution.py:47
  816.4 0.0 copy-done.1
  816.4 0.1 add_bitcast_fusion
  816.6 10.9 %all_to_all.19 = f32[8,20,512]{2,1,0:T(8,128)S(1)} all-to-all(f32[8,20,512]{2,1,0:T(8,128)S(1)} %all_to_all.14), channel_id=1, replica_groups=mesh['silo'=4,'row'=8] {'row'}, dimensions={0} | all-to-all | bytes 655360 | tf_op jit(solution)/shard_map/all_to_all | solution.py:51
  827.5 0.2 copy.9
  827.7 1.0 copy.10
  (5 shorter events, 0.1 us)
Async XLA Ops:
  6.5 70.6 %all-gather.6.cloned.1.call-start = ((), (), s32[]{:S(2)}) async-start(), calls=%async_computation.2 | async-start | bytes 11796480 | tf_op jit(solution)/shard_map/all_gather | solution.py:32
  9.0 121.0 %reduce-scatter.2.cloned.1.call-start = ((), (), s32[]{:S(2)}) async-start(), calls=%async_computation.3 | async-start | bytes 1638400 | tf_op jit(solution)/shard_map/reduce_scatter | solution.py:36
  98.5 593.2 %all-gather.12.cloned.1.call-start = ((), (), s32[]{:S(2)}) async-start(), calls=%async_computation.6 | async-start | bytes 41943040 | tf_op jit(solution)/shard_map/all_gather | solution.py:35
  110.1 611.5 %all-gather.8.cloned.1.call-start = ((), (), s32[]{:S(2)}) async-start(), calls=%async_computation.4 | async-start | bytes 2949120 | tf_op jit(solution)/shard_map/all_gather | solution.py:40
  130.0 660.1 %all-gather.10.cloned.1.call-start = ((), (), s32[]{:S(2)}) async-start(), calls=%async_computation.5 | async-start | bytes 2949120 | tf_op jit(solution)/shard_map/all_gather | solution.py:40
  691.7 30.0 %copy-start = (f32[512,160]{0,1:T(8,128)S(1)}, f32[512,160]{0,1:T(8,128)}, u32[]{:S(2)}) copy-start(f32[512,160]{0,1:T(8,128)} %reduce-scatter.2.cloned.1.call-done) | copy-start | bytes 983044
  759.9 56.5 %copy-start.1 = (f32[512,160]{0,1:T(8,128)S(1)}, f32[512,160]{0,1:T(8,128)}, u32[]{:S(2)}) copy-start(f32[512,160]{0,1:T(8,128)} %multiply_add_fusion) | copy-start | bytes 983044
Sparse Core Ops, SparseCore 0:
  9.2 67.8 all-gather.5
  98.6 31.3 reduce-scatter.1
  131.6 560.0 all-gather.11
  693.4 28.1 all-gather.7
  760.1 29.9 all-gather.9
